TPU v7x, 1024 devices: a whole 8x8x8 slice. The times are simulated.
1024 devices in a mesh: grp: 16 (over y, core), blk: 64 (over z, x).
Axes of the slice: x: 8, y: 8, z: 8, core: 2. Of those that a mesh axis runs over, the one named last changes fastest.
Arguments:
- child_field: bfloat16 [1048576, 384], P(('grp', 'blk')), may hold values from -6 to 6
- child_weight: bfloat16 [1048576], P(('grp', 'blk')), may hold values from 0.099609375 to 0.5
- child_slot: int32 [1048576], P(('grp', 'blk')), may hold values from 0 to 639, as said below
- send_list: int32 [1024, 640], P(('grp', 'blk')), may hold values from -1 to 255, as said below
- theta: float32 [128, 2048], P('grp', 'blk'), may hold values from 0.05 to 0.24
Outputs:
- corrected: float32 [128, 2048, 384], P('grp', 'blk')
Inputs may be any that keep to these rules, and one draw needn't show every extreme that they name: `send_list`: row v lists, for each of its 5 nearby owners k = 0, 1, ... in turn, 128 slots: used slots first, each holding a distinct local parent number e of that owner, then -1 for unused slots; every device uses at least one slot for each nearby owner, and in every device's row one nearby owner has all 128 slots used. `child_slot`: A child's slot is k * 128 + position and is a used slot of its device's row of send_list.
All inputs are finite; a program needn't handle non-finite values.
Results may differ from a plain program's by a relative error of at most 0.0007.
Values sent between devices are 32-bit elements; how exact they have to be, the bound alone decides.
No kernel may reach another device: no remote copies, remote signals or barrier semaphores. Data moves between devices by JAX's collectives and lax.ppermute only.
A program may use at most 32 MiB of HBM per device.

v0:
```python
import jax
import jax.numpy as jnp
from jax import lax
from jax.sharding import PartitionSpec as P

PR = 8
PCOL = 32
HALF = 2
CAP = 128


def from_behind(x, axis, by):
    size = lax.axis_size(axis)
    return lax.ppermute(x, axis, [(i, (i + by) % size) for i in range(size)])


def with_halo(x, sides, width):
    edges = {}
    for axis, dim in sides:
        size, length = (lax.axis_size(axis), x.shape[dim])
        up = [(i, (i + 1) % size) for i in range(size - 1)]
        last = lax.slice_in_dim(x, length - width, length, axis=dim)
        leading = lax.slice_in_dim(x, 0, width, axis=dim)
        edges[dim] = (
            lax.ppermute(last, axis, up),
            lax.ppermute(leading, axis, [(b, a) for a, b in up]),
        )
    done = []
    for _, dim in sides:
        low, high = edges[dim]
        around = [(width, width) if d in done else (0, 0) for d in range(x.ndim)]
        x = jnp.concatenate([jnp.pad(low, around), x, jnp.pad(high, around)], axis=dim)
        done.append(dim)
    return x


def body(child_field, child_weight, child_slot, send_list, theta):
    cells = PR * PCOL
    channels = child_field.shape[1]
    reach = 2 * HALF + 1
    slot_row = send_list.reshape(-1)
    restricted = jnp.zeros((cells, channels), jnp.float32)
    entry = jnp.take(slot_row, child_slot)
    local = child_slot // CAP * cells + entry
    for offset in range(reach):
        ids = offset * cells + jnp.arange(cells, dtype=jnp.int32)
        matrix = jnp.where(
            ids[:, None] == local[None, :], child_weight[None, :], jnp.zeros((), jnp.bfloat16)
        )
        term = jnp.dot(matrix, child_field, preferred_element_type=jnp.float32)
        if offset != HALF:
            term = from_behind(term, "blk", offset - HALF)
        restricted = restricted + term
    restricted = restricted.reshape(PR, PCOL, channels)
    padded = with_halo(restricted, (("grp", 0), ("blk", 1)), 1)
    beside = padded[2:, 1:-1] + padded[:-2, 1:-1] + padded[1:-1, 2:] + padded[1:-1, :-2]
    return restricted + theta[:, :, None] * (beside - 4.0 * restricted)


def solution(mesh):
    return jax.shard_map(
        body,
        mesh=mesh,
        in_specs=(
            P(("grp", "blk"), None),
            P(("grp", "blk")),
            P(("grp", "blk")),
            P(("grp", "blk"), None),
            P("grp", "blk"),
        ),
        out_specs=P("grp", "blk", None),
        check_vma=False,
    )
```

profile of v0, /device:TPU:53, one launch (start us, length us, event | category | flops | bytes accessed | tf_op | source)
XLA Modules:
  0.0 74.4 jit_solution(15700863763865765200)
XLA Ops:
  0.0 0.8 %fusion.38 = s32[1024]{0:T(1024)S(1)} fusion(s32[1024]{0:T(1024)} %param.7), kind=kLoop, calls=%fused_computation.62 | loop fusion | flops 4096 | bytes 8192 | tf_op jit(solution)/shard_map/jit(_take)/gather | solution.py:43
  0.8 0.0 copy-start.1
  0.8 4.5 %gather_fusion = s32[1024]{0:T(1024)S(1)} fusion(s32[640]{0:T(1024)S(1)} %reduce, s32[1024]{0:T(1024)S(1)} %fusion.38), kind=kCustom, calls=%fused_computation | custom fusion | bytes 12288 | tf_op jit(solution)/shard_map/jit(_take)/gather | solution.py:43
  5.4 0.0 copy-start.4
  5.4 0.6 copy-done.4
  6.0 0.5 fusion.1
  6.5 2.2 %collective-permute-start.1 = (f32[256,384]{1,0:T(8,128)S(1)}, f32[256,384]{1,0:T(8,128)S(1)}, u32[]{:S(2)}, u32[]{:S(2)}) collective-permute-start(f32[256,384]{1,0:T(8,128)S(1)} %fusion.1), channel_id=1, source_target_pairs={{0,63},{1,0},{2,1},{3,2},{4,3},{5,4},{6,5},{7,6},{8,7},{9,8},{10,9... | collective-permute-start | bytes 1179656 | tf_op jit(solution)/shard_map/ppermute | solution.py:14
  8.7 0.5 fusion.3
  9.2 3.1 %collective-permute-start.2 = (f32[256,384]{1,0:T(8,128)S(1)}, f32[256,384]{1,0:T(8,128)S(1)}, u32[]{:S(2)}, u32[]{:S(2)}) collective-permute-start(f32[256,384]{1,0:T(8,128)S(1)} %fusion.3), channel_id=1, source_target_pairs={{0,1},{1,2},{2,3},{3,4},{4,5},{5,6},{6,7},{7,8},{8,9},{9,10},{10,1... | collective-permute-start | bytes 1179656 | tf_op jit(solution)/shard_map/ppermute | solution.py:14
  12.4 0.5 fusion.4
  12.8 5.3 %collective-permute-start.3 = (f32[256,384]{1,0:T(8,128)S(1)}, f32[256,384]{1,0:T(8,128)S(1)}, u32[]{:S(2)}, u32[]{:S(2)}) collective-permute-start(f32[256,384]{1,0:T(8,128)S(1)} %fusion.4), channel_id=1, source_target_pairs={{0,2},{1,3},{2,4},{3,5},{4,6},{5,7},{6,8},{7,9},{8,10},{9,11},{10,... | collective-permute-start | bytes 1179656 | tf_op jit(solution)/shard_map/ppermute | solution.py:14
  18.1 0.4 fusion.5
  18.5 14.8 %collective-permute-start = (f32[256,384]{1,0:T(8,128)S(1)}, f32[256,384]{1,0:T(8,128)S(1)}, u32[]{:S(2)}, u32[]{:S(2)}) collective-permute-start(f32[256,384]{1,0:T(8,128)S(1)} %fusion.5), channel_id=1, source_target_pairs={{0,62},{1,63},{2,0},{3,1},{4,2},{5,3},{6,4},{7,5},{8,6},{9,7},{10,... | collective-permute-start | bytes 1179656 | tf_op jit(solution)/shard_map/ppermute | solution.py:14
  33.3 0.0 collective-permute-done.1
  33.4 0.0 collective-permute-done.2
  33.4 19.8 %collective-permute-done.3 = f32[256,384]{1,0:T(8,128)S(1)} collective-permute-done((f32[256,384]{1,0:T(8,128)S(1)}, f32[256,384]{1,0:T(8,128)S(1)}, u32[]{:S(2)}, u32[]{:S(2)}) %collective-permute-start.3) | collective-permute-done | bytes 393248 | tf_op jit(solution)/shard_map/ppermute | solution.py:14
  53.2 0.5 add_add_fusion
  53.7 3.1 %collective-permute-start.4 = (f32[1,32,384]{2,1,0:T(8,128)S(1)}, f32[1,32,384]{2,1,0:T(8,128)S(1)}, u32[]{:S(2)}, u32[]{:S(2)}) collective-permute-start(f32[1,32,384]{2,1,0:T(8,128)S(1)} %get-tuple-element.8), channel_id=1, source_target_pairs={{64,0},{128,64},{192,128},{256,192},{320,256},{384,320},{448,384},... | collective-permute-start | bytes 147464 | tf_op jit(solution)/shard_map/ppermute | solution.py:26
  56.8 4.4 %collective-permute-start.5 = (f32[1,32,384]{2,1,0:T(8,128)S(1)}, f32[1,32,384]{2,1,0:T(8,128)S(1)}, u32[]{:S(2)}, u32[]{:S(2)}) collective-permute-start(f32[1,32,384]{2,1,0:T(8,128)S(1)} %get-tuple-element.7), channel_id=1, source_target_pairs={{0,64},{64,128},{128,192},{192,256},{256,320},{320,384},{384,448},... | collective-permute-start | bytes 147464 | tf_op jit(solution)/shard_map/ppermute | solution.py:25
  61.3 0.0 copy-start.2
  61.3 7.7 %collective-permute-start.6 = (f32[8,1,384]{2,1,0:T(1,128)S(1)}, f32[8,1,384]{2,1,0:T(1,128)S(1)}, u32[]{:S(2)}, u32[]{:S(2)}) collective-permute-start(f32[8,1,384]{2,1,0:T(1,128)S(1)} %get-tuple-element.5), channel_id=1, source_target_pairs={{1,0},{2,1},{3,2},{4,3},{5,4},{6,5},{7,6},{8,7},{9,8},{10,9},{11,1... | collective-permute-start | bytes 36872 | tf_op jit(solution)/shard_map/ppermute | solution.py:26
  69.0 1.9 %collective-permute-start.7 = (f32[8,1,384]{2,1,0:T(1,128)S(1)}, f32[8,1,384]{2,1,0:T(1,128)S(1)}, u32[]{:S(2)}, u32[]{:S(2)}) collective-permute-start(f32[8,1,384]{2,1,0:T(1,128)S(1)} %get-tuple-element.6), channel_id=1, source_target_pairs={{0,1},{1,2},{2,3},{3,4},{4,5},{5,6},{6,7},{7,8},{8,9},{9,10},{10,1... | collective-permute-start | bytes 36872 | tf_op jit(solution)/shard_map/ppermute | solution.py:25
  71.0 2.5 %collective-permute-done.7 = f32[8,1,384]{2,1,0:T(1,128)S(1)} collective-permute-done((f32[8,1,384]{2,1,0:T(1,128)S(1)}, f32[8,1,384]{2,1,0:T(1,128)S(1)}, u32[]{:S(2)}, u32[]{:S(2)}) %collective-permute-start.7) | collective-permute-done | bytes 12320 | tf_op jit(solution)/shard_map/ppermute | solution.py:25
  73.5 0.9 %fusion.20 = f32[8,32,384]{2,1,0:T(8,128)} fusion(f32[8,32,384]{2,1,0:T(8,128)S(1)} %bitcast.11, f32[8,1,384]{2,1,0:T(1,128)S(1)} %collective-permute-done.7, f32[1,32,384]{2,1,0:T(8,128)S(1)} %collective-permute-done.4, f32[1,32,384]{2,1,0:T(8,128)S(1)} %collective-permute-done.5, f32[8,1,384]{2,1,0:T(1,128)S(1)} %collective-permute-done.6, ...), kind=kLoop, calls=%fused_computation.26 | loop fusion | flops 2064384 | bytes 910336 | tf_op jit(solution)/shard_map/add | solution.py:57
  (18 shorter events, 0.1 us)
Async XLA Ops:
  0.0 5.4 %copy-start = (bf16[1024,384]{1,0:T(8,128)(2,1)S(1)}, bf16[1024,384]{1,0:T(8,128)(2,1)}, u32[]{:S(2)}) copy-start(bf16[1024,384]{1,0:T(8,128)(2,1)} %param.5) | copy-start | bytes 2359300
  0.0 0.8 %copy-start.3 = (s32[1,640]{1,0:T(1,128)S(1)}, s32[1,640]{1,0:T(1,128)}, u32[]{:S(2)}) copy-start(s32[1,640]{1,0:T(1,128)} %param.8) | copy-start | bytes 7684
  0.8 4.6 %copy-start.1 = (s32[1024]{0:T(1024)S(1)}, s32[1024]{0:T(1024)}, u32[]{:S(2)}) copy-start(s32[1024]{0:T(1024)} %param.7) | copy-start | bytes 12292
  5.4 0.7 copy-start.4
  6.5 26.8 %collective-permute-start.1 = (f32[256,384]{1,0:T(8,128)S(1)}, f32[256,384]{1,0:T(8,128)S(1)}, u32[]{:S(2)}, u32[]{:S(2)}) collective-permute-start(f32[256,384]{1,0:T(8,128)S(1)} %fusion.1), channel_id=1, source_target_pairs={{0,63},{1,0},{2,1},{3,2},{4,3},{5,4},{6,5},{7,6},{8,7},{9,8},{10,9... | collective-permute-start | bytes 1179656 | tf_op jit(solution)/shard_map/ppermute | solution.py:14
  9.2 24.1 %collective-permute-start.2 = (f32[256,384]{1,0:T(8,128)S(1)}, f32[256,384]{1,0:T(8,128)S(1)}, u32[]{:S(2)}, u32[]{:S(2)}) collective-permute-start(f32[256,384]{1,0:T(8,128)S(1)} %fusion.3), channel_id=1, source_target_pairs={{0,1},{1,2},{2,3},{3,4},{4,5},{5,6},{6,7},{7,8},{8,9},{9,10},{10,1... | collective-permute-start | bytes 1179656 | tf_op jit(solution)/shard_map/ppermute | solution.py:14
  12.8 40.4 %collective-permute-start.3 = (f32[256,384]{1,0:T(8,128)S(1)}, f32[256,384]{1,0:T(8,128)S(1)}, u32[]{:S(2)}, u32[]{:S(2)}) collective-permute-start(f32[256,384]{1,0:T(8,128)S(1)} %fusion.4), channel_id=1, source_target_pairs={{0,2},{1,3},{2,4},{3,5},{4,6},{5,7},{6,8},{7,9},{8,10},{9,11},{10,... | collective-permute-start | bytes 1179656 | tf_op jit(solution)/shard_map/ppermute | solution.py:14
  18.5 34.7 %collective-permute-start = (f32[256,384]{1,0:T(8,128)S(1)}, f32[256,384]{1,0:T(8,128)S(1)}, u32[]{:S(2)}, u32[]{:S(2)}) collective-permute-start(f32[256,384]{1,0:T(8,128)S(1)} %fusion.5), channel_id=1, source_target_pairs={{0,62},{1,63},{2,0},{3,1},{4,2},{5,3},{6,4},{7,5},{8,6},{9,7},{10,... | collective-permute-start | bytes 1179656 | tf_op jit(solution)/shard_map/ppermute | solution.py:14
  53.7 19.8 %collective-permute-start.4 = (f32[1,32,384]{2,1,0:T(8,128)S(1)}, f32[1,32,384]{2,1,0:T(8,128)S(1)}, u32[]{:S(2)}, u32[]{:S(2)}) collective-permute-start(f32[1,32,384]{2,1,0:T(8,128)S(1)} %get-tuple-element.8), channel_id=1, source_target_pairs={{64,0},{128,64},{192,128},{256,192},{320,256},{384,320},{448,384},... | collective-permute-start | bytes 147464 | tf_op jit(solution)/shard_map/ppermute | solution.py:26
  56.8 16.7 %collective-permute-start.5 = (f32[1,32,384]{2,1,0:T(8,128)S(1)}, f32[1,32,384]{2,1,0:T(8,128)S(1)}, u32[]{:S(2)}, u32[]{:S(2)}) collective-permute-start(f32[1,32,384]{2,1,0:T(8,128)S(1)} %get-tuple-element.7), channel_id=1, source_target_pairs={{0,64},{64,128},{128,192},{192,256},{256,320},{320,384},{384,448},... | collective-permute-start | bytes 147464 | tf_op jit(solution)/shard_map/ppermute | solution.py:25
  61.3 12.2 %copy-start.2 = (f32[8,32]{1,0:T(8,128)S(1)}, f32[8,32]{1,0:T(8,128)}, u32[]{:S(2)}) copy-start(f32[8,32]{1,0:T(8,128)} %param.9) | copy-start | bytes 3076
  61.3 9.7 %collective-permute-start.6 = (f32[8,1,384]{2,1,0:T(1,128)S(1)}, f32[8,1,384]{2,1,0:T(1,128)S(1)}, u32[]{:S(2)}, u32[]{:S(2)}) collective-permute-start(f32[8,1,384]{2,1,0:T(1,128)S(1)} %get-tuple-element.5), channel_id=1, source_target_pairs={{1,0},{2,1},{3,2},{4,3},{5,4},{6,5},{7,6},{8,7},{9,8},{10,9},{11,1... | collective-permute-start | bytes 36872 | tf_op jit(solution)/shard_map/ppermute | solution.py:26
  69.0 4.4 %collective-permute-start.7 = (f32[8,1,384]{2,1,0:T(1,128)S(1)}, f32[8,1,384]{2,1,0:T(1,128)S(1)}, u32[]{:S(2)}, u32[]{:S(2)}) collective-permute-start(f32[8,1,384]{2,1,0:T(1,128)S(1)} %get-tuple-element.6), channel_id=1, source_target_pairs={{0,1},{1,2},{2,3},{3,4},{4,5},{5,6},{6,7},{7,8},{8,9},{9,10},{10,1... | collective-permute-start | bytes 36872 | tf_op jit(solution)/shard_map/ppermute | solution.py:25
where the time goes:
time: 74.8 us; the launch traced here: 74.4 us
  starting transfers between devices  42.5 us (57%)
  waiting for transfers between devices  22.3 us (30%)
  local copies, waits for them, and re-layouts  5.23 us (7%)
  matrix products  2.38 us (3%)
  other arithmetic  1.74 us (2%)
    ppermute x4, starting transfers between devices, from_behind(): return lax.ppermute(x, axis, [(i, (i + by) % size) for i in range(size)])  25.3 us
    ppermute x4, waiting for transfers between devices, from_behind(): return lax.ppermute(x, axis, [(i, (i + by) % size) for i in range(size)])  19.8 us
    ppermute x2, starting transfers between devices, with_halo(): lax.ppermute(leading, axis, [(b, a) for a, b in up])  10.8 us
    ppermute x2, starting transfers between devices, with_halo(): lax.ppermute(last, axis, up)  6.35 us
    gather x1, local copies, waits for them, and re-layouts, body(): entry = jnp.take(slot_row, child_slot)  4.53 us
    ppermute x2, waiting for transfers between devices, with_halo(): lax.ppermute(last, axis, up)  2.5 us
    dot_general x5, matrix products, body(): term = jnp.dot(matrix, child_field, preferred_element_type=jnp.float32)  2.38 us
  transfers between devices with their start and end apart: 8, of which 2 were waited for; matrix products, arithmetic and copies ran while one was open for 2% of the time, Pallas kernels for 0%

commit v1 on v0

v1 whole, which is shorter than its diff:
```python
import functools

import jax
import jax.numpy as jnp
from jax import lax
from jax.experimental import pallas as pl
from jax.experimental.pallas import tpu as pltpu
from jax.sharding import PartitionSpec as P


PR = 8
PCOL = 32
CELLS = PR * PCOL
HALF = 2
REACH = 2 * HALF + 1
CAP = 128
LANES = 128
F32 = jnp.float32
BF16 = jnp.bfloat16

VMEM = pl.BlockSpec(memory_space=pltpu.VMEM)
SMEM = pl.BlockSpec(memory_space=pltpu.SMEM)


def shift(x, axis, by):
    size = lax.axis_size(axis)
    return lax.ppermute(x, axis, [(i, (i + by) % size) for i in range(size)])


def step(x, axis, by):
    size = lax.axis_size(axis)
    return lax.ppermute(x, axis, [(i, i + by) for i in range(size) if 0 <= i + by < size])


def swap(x, axis, first):
    size = lax.axis_size(axis)
    pairs = []
    for i in range(first, size - 1, 2):
        pairs += [(i, i + 1), (i + 1, i)]
    return lax.ppermute(x, axis, pairs)


def slot_sums(field, weight, slot, k):
    ids = k * CAP + lax.broadcasted_iota(jnp.int32, (CAP, slot.shape[1]), 0)
    matrix = jnp.where(ids == slot, weight, 0.0).astype(BF16)
    return jnp.dot(matrix, field, preferred_element_type=F32)


def spread(matrix, sums):
    high = sums.astype(BF16)
    low = (sums - high.astype(F32)).astype(BF16)
    both = jnp.dot(matrix, high, preferred_element_type=F32)
    return both + jnp.dot(matrix, low, preferred_element_type=F32)


def send_kernel(ks, field_ref, weight_ref, slot_ref, list_ref, *out_refs):
    for k, out_ref in zip(ks, out_refs):
        sums = slot_sums(field_ref[...], weight_ref[...], slot_ref[...], k)
        for j in range(sums.shape[1] // LANES):
            out_ref[j * CAP : (j + 1) * CAP, :] = sums[:, j * LANES : (j + 1) * LANES]
        row = list_ref[k : k + 1, :].astype(F32)
        out_ref[sums.shape[1] : sums.shape[1] + 8, :] = jnp.broadcast_to(row, (8, LANES))


def own_kernel(field_ref, weight_ref, slot_ref, list_ref, theta_ref, out_ref, wide_ref):
    sums = slot_sums(field_ref[...], weight_ref[...], slot_ref[...], HALF)
    row = list_ref[HALF : HALF + 1, :]
    matrix = jnp.where(lax.broadcasted_iota(jnp.int32, (CELLS, CAP), 0) == row, 1.0, 0.0).astype(BF16)
    out_ref[...] = spread(matrix, sums)
    here = lax.broadcasted_iota(jnp.int32, (PCOL, PCOL), 0) == lax.broadcasted_iota(jnp.int32, (PCOL, PCOL), 1)
    for r in range(PR):
        column = jnp.sum(jnp.where(here, theta_ref[r : r + 1, :], 0.0), axis=1, keepdims=True)
        wide_ref[r * PCOL : (r + 1) * PCOL, :] = jnp.broadcast_to(column, (PCOL, LANES))


def gather_kernel(odd_ref, own_ref, *refs):
    messages, (out_ref, chip_ref, side_ref, last_ref, first_ref) = refs[:-5], refs[-5:]
    channels = own_ref.shape[1]
    cells = lax.broadcasted_iota(jnp.int32, (CELLS, CAP), 0).astype(F32)
    for j in range(channels // LANES):
        total = own_ref[:, j * LANES : (j + 1) * LANES]
        for msg in messages:
            matrix = jnp.where(cells == msg[channels : channels + 1, :], 1.0, 0.0).astype(BF16)
            total = total + spread(matrix, msg[j * CAP : (j + 1) * CAP, :])
        out_ref[:, j * LANES : (j + 1) * LANES] = total
    odd = odd_ref[0]
    tail = (PR - 1) * PCOL
    chip_ref[...] = out_ref[pl.ds(pl.multiple_of((1 - odd) * tail, PCOL), PCOL), :]
    side_ref[...] = out_ref[pl.ds(pl.multiple_of(odd * tail, PCOL), PCOL), :]
    for r in range(PR):
        last_ref[r : r + 1, :] = out_ref[(r + 1) * PCOL - 1 : (r + 1) * PCOL, :]
        first_ref[r : r + 1, :] = out_ref[r * PCOL : r * PCOL + 1, :]


def final_kernel(odd_ref, own_ref, wide_ref, chip_ref, side_ref, left_ref, right_ref, out_ref):
    odd = odd_ref[0] == 1
    for r in range(PR):
        low, high = r * PCOL, (r + 1) * PCOL
        here = own_ref[low:high, :]
        if r == 0:
            above = jnp.where(odd, chip_ref[...], side_ref[...])
        else:
            above = own_ref[low - PCOL : low, :]
        if r == PR - 1:
            below = jnp.where(odd, side_ref[...], chip_ref[...])
        else:
            below = own_ref[high : high + PCOL, :]
        west = jnp.concatenate([left_ref[r : r + 1, :], here[:-1]], axis=0)
        east = jnp.concatenate([here[1:], right_ref[r : r + 1, :]], axis=0)
        factor = jnp.concatenate([wide_ref[low:high, :]] * (here.shape[1] // LANES), axis=1)
        out_ref[low:high, :] = here + factor * (below + above + east + west - 4.0 * here)


def struct(shape, dtype=F32):
    return jax.ShapeDtypeStruct(shape, dtype)


def call(kernel, outs, specs, flops):
    return pl.pallas_call(
        kernel,
        out_shape=outs,
        in_specs=specs,
        out_specs=jax.tree.map(lambda _: VMEM, outs),
        compiler_params=pltpu.CompilerParams(vmem_limit_bytes=16 * 1024 * 1024),
        cost_estimate=pl.CostEstimate(flops=flops, bytes_accessed=1000000, transcendentals=0),
    )


def body(child_field, child_weight, child_slot, send_list, theta):
    children, channels = child_field.shape
    weight = child_weight.astype(F32).reshape(1, children)
    slot = child_slot.reshape(1, children)
    listed = send_list.reshape(REACH, CAP)
    odd = (lax.axis_index("grp") % 2).reshape(1).astype(jnp.int32)
    message = struct((channels + 8, LANES))
    work = 2 * CAP * children * channels

    def sends(ks):
        kernel = functools.partial(send_kernel, ks)
        outs = [message] * len(ks)
        return call(kernel, outs, [VMEM] * 4, work * len(ks))(child_field, weight, slot, listed)

    arrived = []
    for k in (4, 3, 1, 0):
        (msg,) = sends((k,))
        arrived.append(shift(msg, "blk", k - HALF))
    own, wide = call(own_kernel, [struct((CELLS, channels)), struct((CELLS, LANES))], [VMEM] * 5, 2 * work)(
        child_field, weight, slot, listed, theta
    )
    outs = [struct((CELLS, channels))] + [struct((PCOL, channels))] * 2 + [struct((PR, channels))] * 2
    restricted, chip, side, last, first = call(gather_kernel, outs, [SMEM] + [VMEM] * 5, work)(odd, own, *arrived)
    side = swap(side, "grp", 1)
    left = step(last, "blk", 1)
    right = step(first, "blk", -1)
    chip = swap(chip, "grp", 0)
    out = call(final_kernel, struct((CELLS, channels)), [SMEM] + [VMEM] * 6, work)(
        odd, restricted, wide, chip, side, left, right
    )
    return out.reshape(PR, PCOL, channels)


def solution(mesh):
    return jax.shard_map(
        body,
        mesh=mesh,
        in_specs=(
            P(("grp", "blk"), None),
            P(("grp", "blk")),
            P(("grp", "blk")),
            P(("grp", "blk"), None),
            P("grp", "blk"),
        ),
        out_specs=P("grp", "blk", None),
        check_vma=False,
    )
```

time: 74.8 us -> 55.6 us (0.74)
  the two profiles are of different devices: /device:TPU:53 before, /device:TPU:49 now
where the time goes in v1:
time: 55.6 us; the launch traced here: 55.1 us
  starting transfers between devices  42.5 us (76%)
  waiting for transfers between devices  6.04 us (11%)
  Pallas kernels  3.23 us (6%)
  local copies, waits for them, and re-layouts  2.49 us (4%)
  other arithmetic  0.71 us (1%)
    ppermute x4, starting transfers between devices, shift(): return lax.ppermute(x, axis, [(i, (i + by) % size) for i in range(size)])  27.6 us
    ppermute x2, starting transfers between devices, swap(): return lax.ppermute(x, axis, pairs)  8.2 us
    ppermute x2, starting transfers between devices, step(): lax.ppermute(x, axis, [(i, i + by) for i in range(size) if 0 <= i + by <...  6.71 us
    ppermute x2, waiting for transfers between devices, step(): lax.ppermute(x, axis, [(i, i + by) for i in range(size) if 0 <= i + by <...  3.13 us
    ppermute x4, waiting for transfers between devices, shift(): return lax.ppermute(x, axis, [(i, (i + by) % size) for i in range(size)])  2.9 us
    unnamed x10, local copies, waits for them, and re-layouts  2.49 us
    pallas_call x4, Pallas kernels, sends(): call(kernel, outs, [VMEM] * 4, work * len(ks))  1.19 us
  transfers between devices with their start and end apart: 8, of which 3 were waited for; matrix products, arithmetic and copies ran while one was open for 0% of the time, Pallas kernels for 3%

profile of v1, /device:TPU:49, one launch (start us, length us, event | category | flops | bytes accessed | tf_op | source)
XLA Modules:
  0.0 55.1 jit_solution(941083149061371456)
XLA Ops:
  0.0 0.7 %reshape.23 = f32[1024]{0:T(1024)S(1)} convert(bf16[1024]{0:T(1024)(128)(2,1)} %param.6) | non-fusion elementwise | flops 1024 | bytes 6144 | tf_op jit(solution)/shard_map/reshape | solution.py:131
  0.7 0.0 copy-start.2
  0.7 0.7 %copy-done.2 = s32[1024]{0:T(1024)S(1)} copy-done((s32[1024]{0:T(1024)S(1)}, s32[1024]{0:T(1024)}, u32[]{:S(2)}) %copy-start.2) | copy-done | bytes 4120
  1.4 1.1 %copy-done = bf16[1024,384]{1,0:T(8,128)(2,1)S(1)} copy-done((bf16[1024,384]{1,0:T(8,128)(2,1)S(1)}, bf16[1024,384]{1,0:T(8,128)(2,1)}, u32[]{:S(2)}) %copy-start) | copy-done | bytes 786456
  2.5 0.3 shard_map.56
  2.8 4.0 %collective-permute-start = (f32[392,128]{1,0:T(8,128)S(1)}, f32[392,128]{1,0:T(8,128)S(1)}, u32[]{:S(2)}, u32[]{:S(2)}) collective-permute-start(f32[392,128]{1,0:T(8,128)S(1)} %shard_map.56), channel_id=1, source_target_pairs={{0,2},{1,3},{2,4},{3,5},{4,6},{5,7},{6,8},{7,9},{8,10},{9,11},{10,... | collective-permute-start | bytes 602120 | tf_op jit(solution)/shard_map/ppermute | solution.py:27
  6.9 0.3 shard_map.57
  7.2 0.0 copy-start.1
  7.2 3.2 %collective-permute-start.1 = (f32[392,128]{1,0:T(8,128)S(1)}, f32[392,128]{1,0:T(8,128)S(1)}, u32[]{:S(2)}, u32[]{:S(2)}) collective-permute-start(f32[392,128]{1,0:T(8,128)S(1)} %shard_map.57), channel_id=1, source_target_pairs={{0,1},{1,2},{2,3},{3,4},{4,5},{5,6},{6,7},{7,8},{8,9},{9,10},{10,1... | collective-permute-start | bytes 602120 | tf_op jit(solution)/shard_map/ppermute | solution.py:27
  10.5 0.3 shard_map.58
  10.8 16.0 %collective-permute-start.2 = (f32[392,128]{1,0:T(8,128)S(1)}, f32[392,128]{1,0:T(8,128)S(1)}, u32[]{:S(2)}, u32[]{:S(2)}) collective-permute-start(f32[392,128]{1,0:T(8,128)S(1)} %shard_map.58), channel_id=1, source_target_pairs={{0,63},{1,0},{2,1},{3,2},{4,3},{5,4},{6,5},{7,6},{8,7},{9,8},{10,9... | collective-permute-start | bytes 602120 | tf_op jit(solution)/shard_map/ppermute | solution.py:27
  26.8 0.3 shard_map.59
  27.1 4.3 %collective-permute-start.3 = (f32[392,128]{1,0:T(8,128)S(1)}, f32[392,128]{1,0:T(8,128)S(1)}, u32[]{:S(2)}, u32[]{:S(2)}) collective-permute-start(f32[392,128]{1,0:T(8,128)S(1)} %shard_map.59), channel_id=1, source_target_pairs={{0,62},{1,63},{2,0},{3,1},{4,2},{5,3},{6,4},{7,5},{8,6},{9,7},{10,... | collective-permute-start | bytes 602120 | tf_op jit(solution)/shard_map/ppermute | solution.py:27
  31.4 0.7 %copy-done.3 = f32[8,32]{1,0:T(8,128)S(1)} copy-done((f32[8,32]{1,0:T(8,128)S(1)}, f32[8,32]{1,0:T(8,128)}, u32[]{:S(2)}) %copy-start.3) | copy-done | bytes 1048
  32.1 0.6 shard_map.55
  32.6 2.8 %collective-permute-done.1.refs_1_ = f32[392,128]{1,0:T(8,128)S(1)} collective-permute-done((f32[392,128]{1,0:T(8,128)S(1)}, f32[392,128]{1,0:T(8,128)S(1)}, u32[]{:S(2)}, u32[]{:S(2)}) %collective-permute-start.1) | collective-permute-done | bytes 200736 | tf_op jit(solution)/shard_map/ppermute | solution.py:27
  35.5 0.1 collective-permute-done.3.refs_3_
  35.5 0.6 %shard_map.60 = (f32[256,384]{1,0:T(8,128)S(1)}, f32[32,384]{1,0:T(8,128)S(1)}, f32[32,384]{1,0:T(8,128)S(1)}, f32[8,384]{1,0:T(8,128)S(1)}, f32[8,384]{1,0:T(8,128)S(1)}) custom-call(s32[1]{0:T(128)} %bitcast.odd_ref, f32[256,384]{1,0:T(8,128)S(1)} %get-tuple-element.12.own_ref, f32[392,128]{1,0:T(8,128)S(1)} %collective-permute-done.refs_0_, ...), custom_call_target="tpu_custom_call" | custom-call | flops 100663296 | bytes 1000000 | tf_op jit(solution)/shard_map/pallas_call | solution.py:151
  36.1 3.8 %collective-permute-start.4 = (f32[32,384]{1,0:T(8,128)S(1)}, f32[32,384]{1,0:T(8,128)S(1)}, u32[]{:S(2)}, u32[]{:S(2)}) collective-permute-start(f32[32,384]{1,0:T(8,128)S(1)} %get-tuple-element.15), channel_id=1, source_target_pairs={{0,64},{64,0},{128,192},{192,128},{256,320},{320,256},{384,448},{4... | collective-permute-start | bytes 147464 | tf_op jit(solution)/shard_map/ppermute | solution.py:40
  39.9 4.4 %collective-permute-start.5 = (f32[32,384]{1,0:T(8,128)S(1)}, f32[32,384]{1,0:T(8,128)S(1)}, u32[]{:S(2)}, u32[]{:S(2)}) collective-permute-start(f32[32,384]{1,0:T(8,128)S(1)} %get-tuple-element.16), channel_id=1, source_target_pairs={{64,128},{128,64},{192,256},{256,192},{320,384},{384,320},{448,512... | collective-permute-start | bytes 147464 | tf_op jit(solution)/shard_map/ppermute | solution.py:40
  44.3 5.4 %collective-permute-start.6 = (f32[8,384]{1,0:T(8,128)S(1)}, f32[8,384]{1,0:T(8,128)S(1)}, u32[]{:S(2)}, u32[]{:S(2)}) collective-permute-start(f32[8,384]{1,0:T(8,128)S(1)} %get-tuple-element.17), channel_id=1, source_target_pairs={{0,1},{1,2},{2,3},{3,4},{4,5},{5,6},{6,7},{7,8},{8,9},{9,10},{10,1... | collective-permute-start | bytes 36872 | tf_op jit(solution)/shard_map/ppermute | solution.py:32
  49.8 1.3 %collective-permute-start.7 = (f32[8,384]{1,0:T(8,128)S(1)}, f32[8,384]{1,0:T(8,128)S(1)}, u32[]{:S(2)}, u32[]{:S(2)}) collective-permute-start(f32[8,384]{1,0:T(8,128)S(1)} %get-tuple-element.18), channel_id=1, source_target_pairs={{1,0},{2,1},{3,2},{4,3},{5,4},{6,5},{7,6},{8,7},{9,8},{10,9},{11,1... | collective-permute-start | bytes 36872 | tf_op jit(solution)/shard_map/ppermute | solution.py:32
  51.1 3.1 %collective-permute-done.7.right_ref = f32[8,384]{1,0:T(8,128)S(1)} collective-permute-done((f32[8,384]{1,0:T(8,128)S(1)}, f32[8,384]{1,0:T(8,128)S(1)}, u32[]{:S(2)}, u32[]{:S(2)}) %collective-permute-start.7) | collective-permute-done | bytes 12320 | tf_op jit(solution)/shard_map/ppermute | solution.py:32
  54.2 0.9 %shard_map.61 = f32[256,384]{1,0:T(8,128)} custom-call(s32[1]{0:T(128)} %bitcast.odd_ref, f32[256,384]{1,0:T(8,128)S(1)} %get-tuple-element.13.own_ref, f32[256,128]{1,0:T(8,128)S(1)} %get-tuple-element.14.wide_ref, f32[32,384]{1,0:T(8,128)S(1)} %collective-permute-done.4.chip_ref, f32[32,384]{1,0:T(8,128)S(1)} %collective-permute-done.5.side_ref, ...), custom_call_target="tpu_custom_call" | custom-call | flops 100663296 | bytes 1000000 | tf_op jit(solution)/shard_map/pallas_call | solution.py:156
  (11 shorter events, 0.0 us)
Async XLA Ops:
  0.0 0.7 %copy-start.4 = (s32[1,640]{1,0:T(1,128)S(1)}, s32[1,640]{1,0:T(1,128)}, u32[]{:S(2)}) copy-start(s32[1,640]{1,0:T(1,128)} %param.8) | copy-start | bytes 7684
  0.7 0.7 %copy-start.2 = (s32[1024]{0:T(1024)S(1)}, s32[1024]{0:T(1024)}, u32[]{:S(2)}) copy-start(s32[1024]{0:T(1024)} %param.7) | copy-start | bytes 12292
  1.4 1.1 %copy-start = (bf16[1024,384]{1,0:T(8,128)(2,1)S(1)}, bf16[1024,384]{1,0:T(8,128)(2,1)}, u32[]{:S(2)}) copy-start(bf16[1024,384]{1,0:T(8,128)(2,1)} %field_ref.9) | copy-start | bytes 2359300
  2.8 29.8 %collective-permute-start = (f32[392,128]{1,0:T(8,128)S(1)}, f32[392,128]{1,0:T(8,128)S(1)}, u32[]{:S(2)}, u32[]{:S(2)}) collective-permute-start(f32[392,128]{1,0:T(8,128)S(1)} %shard_map.56), channel_id=1, source_target_pairs={{0,2},{1,3},{2,4},{3,5},{4,6},{5,7},{6,8},{7,9},{8,10},{9,11},{10,... | collective-permute-start | bytes 602120 | tf_op jit(solution)/shard_map/ppermute | solution.py:27
  7.2 24.2 %copy-start.1 = (bf16[1024,384]{1,0:T(8,128)(2,1)S(1)}, bf16[1024,384]{1,0:T(8,128)(2,1)}, u32[]{:S(2)}) copy-start(bf16[1024,384]{1,0:T(8,128)(2,1)} %field_ref.9) | copy-start | bytes 2359300
  7.2 28.3 %collective-permute-start.1 = (f32[392,128]{1,0:T(8,128)S(1)}, f32[392,128]{1,0:T(8,128)S(1)}, u32[]{:S(2)}, u32[]{:S(2)}) collective-permute-start(f32[392,128]{1,0:T(8,128)S(1)} %shard_map.57), channel_id=1, source_target_pairs={{0,1},{1,2},{2,3},{3,4},{4,5},{5,6},{6,7},{7,8},{8,9},{9,10},{10,1... | collective-permute-start | bytes 602120 | tf_op jit(solution)/shard_map/ppermute | solution.py:27
  10.8 24.7 %collective-permute-start.2 = (f32[392,128]{1,0:T(8,128)S(1)}, f32[392,128]{1,0:T(8,128)S(1)}, u32[]{:S(2)}, u32[]{:S(2)}) collective-permute-start(f32[392,128]{1,0:T(8,128)S(1)} %shard_map.58), channel_id=1, source_target_pairs={{0,63},{1,0},{2,1},{3,2},{4,3},{5,4},{6,5},{7,6},{8,7},{9,8},{10,9... | collective-permute-start | bytes 602120 | tf_op jit(solution)/shard_map/ppermute | solution.py:27
  27.1 8.4 %collective-permute-start.3 = (f32[392,128]{1,0:T(8,128)S(1)}, f32[392,128]{1,0:T(8,128)S(1)}, u32[]{:S(2)}, u32[]{:S(2)}) collective-permute-start(f32[392,128]{1,0:T(8,128)S(1)} %shard_map.59), channel_id=1, source_target_pairs={{0,62},{1,63},{2,0},{3,1},{4,2},{5,3},{6,4},{7,5},{8,6},{9,7},{10,... | collective-permute-start | bytes 602120 | tf_op jit(solution)/shard_map/ppermute | solution.py:27
  31.4 0.7 %copy-start.3 = (f32[8,32]{1,0:T(8,128)S(1)}, f32[8,32]{1,0:T(8,128)}, u32[]{:S(2)}) copy-start(f32[8,32]{1,0:T(8,128)} %theta_ref.1) | copy-start | bytes 3076
  36.1 18.1 %collective-permute-start.4 = (f32[32,384]{1,0:T(8,128)S(1)}, f32[32,384]{1,0:T(8,128)S(1)}, u32[]{:S(2)}, u32[]{:S(2)}) collective-permute-start(f32[32,384]{1,0:T(8,128)S(1)} %get-tuple-element.15), channel_id=1, source_target_pairs={{0,64},{64,0},{128,192},{192,128},{256,320},{320,256},{384,448},{4... | collective-permute-start | bytes 147464 | tf_op jit(solution)/shard_map/ppermute | solution.py:40
  39.9 14.3 %collective-permute-start.5 = (f32[32,384]{1,0:T(8,128)S(1)}, f32[32,384]{1,0:T(8,128)S(1)}, u32[]{:S(2)}, u32[]{:S(2)}) collective-permute-start(f32[32,384]{1,0:T(8,128)S(1)} %get-tuple-element.16), channel_id=1, source_target_pairs={{64,128},{128,64},{192,256},{256,192},{320,384},{384,320},{448,512... | collective-permute-start | bytes 147464 | tf_op jit(solution)/shard_map/ppermute | solution.py:40
  44.3 6.7 %collective-permute-start.6 = (f32[8,384]{1,0:T(8,128)S(1)}, f32[8,384]{1,0:T(8,128)S(1)}, u32[]{:S(2)}, u32[]{:S(2)}) collective-permute-start(f32[8,384]{1,0:T(8,128)S(1)} %get-tuple-element.17), channel_id=1, source_target_pairs={{0,1},{1,2},{2,3},{3,4},{4,5},{5,6},{6,7},{7,8},{8,9},{9,10},{10,1... | collective-permute-start | bytes 36872 | tf_op jit(solution)/shard_map/ppermute | solution.py:32
  49.8 4.4 %collective-permute-start.7 = (f32[8,384]{1,0:T(8,128)S(1)}, f32[8,384]{1,0:T(8,128)S(1)}, u32[]{:S(2)}, u32[]{:S(2)}) collective-permute-start(f32[8,384]{1,0:T(8,128)S(1)} %get-tuple-element.18), channel_id=1, source_target_pairs={{1,0},{2,1},{3,2},{4,3},{5,4},{6,5},{7,6},{8,7},{9,8},{10,9},{11,1... | collective-permute-start | bytes 36872 | tf_op jit(solution)/shard_map/ppermute | solution.py:32

commit v2 on v1

v2 whole, which is shorter than its diff:
```python
import functools

import jax
import jax.numpy as jnp
from jax import lax
from jax.experimental import pallas as pl
from jax.experimental.pallas import tpu as pltpu
from jax.sharding import PartitionSpec as P


PR = 8
PCOL = 32
CELLS = PR * PCOL
HALF = 2
CAP = 128
LANES = 128
F32 = jnp.float32
BF16 = jnp.bfloat16

VMEM = pl.BlockSpec(memory_space=pltpu.VMEM)
SMEM = pl.BlockSpec(memory_space=pltpu.SMEM)


def swap_open(x, axis, first):
    size = lax.axis_size(axis)
    pairs = []
    for i in range(first, size - 1, 2):
        pairs += [(i, i + 1), (i + 1, i)]
    return lax.ppermute(x, axis, pairs)


def iota(shape, dim):
    return lax.broadcasted_iota(jnp.int32, shape, dim)


def slot_sums(weight_ref, slot_ref, field_ref, k):
    ids = k * CAP + iota((CAP, LANES), 0)
    weight, slot = weight_ref[...].astype(F32), slot_ref[...]
    blocks = [
        jnp.where(ids == slot[j : j + 1, :], weight[j : j + 1, :], 0.0).astype(BF16) for j in range(slot.shape[0])
    ]
    return jnp.dot(jnp.concatenate(blocks, axis=1), field_ref[...], preferred_element_type=F32)


def one_hot(ids, row):
    return jnp.where(ids == row, 1.0, 0.0).astype(BF16)


def spread(matrix, sums):
    high = sums.astype(BF16)
    low = (sums - high.astype(F32)).astype(BF16)
    both = jnp.dot(matrix, high, preferred_element_type=F32)
    return both + jnp.dot(matrix, low, preferred_element_type=F32)


def send_kernel(choose, blk_ref, weight_ref, slot_ref, field_ref, list_ref, out_ref):
    k = choose(blk_ref[0])
    at = pl.ds(pl.multiple_of(k * CAP, CAP), CAP)
    sums = slot_sums(weight_ref, slot_ref, field_ref, k)
    channels = sums.shape[1]
    for j in range(channels // LANES):
        out_ref[j * CAP : (j + 1) * CAP, :] = sums[:, j * LANES : (j + 1) * LANES]
    out_ref[channels : channels + 8, :] = jnp.broadcast_to(list_ref[:, at].astype(F32), (8, LANES))


def own_kernel(weight_ref, slot_ref, field_ref, list_ref, theta_ref, out_ref, wide_ref):
    mine = slice(HALF * CAP, (HALF + 1) * CAP)
    sums = slot_sums(weight_ref, slot_ref, field_ref, HALF)
    out_ref[...] = spread(one_hot(iota((CELLS, CAP), 0), list_ref[:, mine]), sums)
    here = iota((PCOL, PCOL), 0) == iota((PCOL, PCOL), 1)
    for r in range(PR):
        column = jnp.sum(jnp.where(here, theta_ref[r : r + 1, :], 0.0), axis=1, keepdims=True)
        wide_ref[r * PCOL : (r + 1) * PCOL, :] = jnp.broadcast_to(column, (PCOL, LANES))


def gather_kernel(grp_ref, own_ref, *refs):
    messages, (out_ref, chip_ref, side_ref, last_ref, first_ref) = refs[:-5], refs[-5:]
    channels = own_ref.shape[1]
    cells = iota((CELLS, CAP), 0).astype(F32)
    matrices = [one_hot(cells, msg[channels : channels + 1, :]) for msg in messages]
    for j in range(channels // LANES):
        lanes = slice(j * LANES, (j + 1) * LANES)
        total = own_ref[:, lanes]
        for matrix, msg in zip(matrices, messages):
            total = total + spread(matrix, msg[j * CAP : (j + 1) * CAP, :])
        out_ref[:, lanes] = total
    odd = grp_ref[0] % 2
    tail = (PR - 1) * PCOL
    chip_ref[...] = out_ref[pl.ds(pl.multiple_of((1 - odd) * tail, PCOL), PCOL), :]
    side_ref[...] = out_ref[pl.ds(pl.multiple_of(odd * tail, PCOL), PCOL), :]
    for r in range(PR):
        last_ref[r : r + 1, :] = out_ref[(r + 1) * PCOL - 1 : (r + 1) * PCOL, :]
        first_ref[r : r + 1, :] = out_ref[r * PCOL : r * PCOL + 1, :]


def final_kernel(grp_ref, own_ref, wide_ref, chip_ref, side_ref, left_ref, right_ref, out_ref):
    odd = grp_ref[0] % 2 == 1
    for r in range(PR):
        low, high = r * PCOL, (r + 1) * PCOL
        here = own_ref[low:high, :]
        if r == 0:
            above = jnp.where(odd, chip_ref[...], side_ref[...])
        else:
            above = own_ref[low - PCOL : low, :]
        if r == PR - 1:
            below = jnp.where(odd, side_ref[...], chip_ref[...])
        else:
            below = own_ref[high : high + PCOL, :]
        west = jnp.concatenate([left_ref[r : r + 1, :], here[:-1]], axis=0)
        east = jnp.concatenate([here[1:], right_ref[r : r + 1, :]], axis=0)
        factor = jnp.concatenate([wide_ref[low:high, :]] * (here.shape[1] // LANES), axis=1)
        out_ref[low:high, :] = here + factor * (below + above + east + west - 4.0 * here)


def struct(shape, dtype=F32):
    return jax.ShapeDtypeStruct(shape, dtype)


def call(kernel, outs, specs, flops, scratch=(), grant=8):
    return pl.pallas_call(
        kernel,
        out_shape=outs,
        in_specs=specs,
        out_specs=jax.tree.map(lambda _: VMEM, outs),
        scratch_shapes=scratch,
        compiler_params=pltpu.CompilerParams(vmem_limit_bytes=grant * 1024 * 1024),
        cost_estimate=pl.CostEstimate(flops=flops, bytes_accessed=1000000, transcendentals=0),
    )


def body(child_field, child_weight, child_slot, send_list, theta):
    children, channels = child_field.shape
    size = lax.axis_size("blk")
    blk = lax.axis_index("blk").reshape(1).astype(jnp.int32)
    grp = lax.axis_index("grp").reshape(1).astype(jnp.int32)
    weight = child_weight.reshape(children // LANES, LANES)
    slot = child_slot.reshape(children // LANES, LANES)
    work = 2 * CAP * children * channels
    message = struct((channels + 8, LANES))

    def trade(choose, pairs):
        kernel = functools.partial(send_kernel, choose)
        msg = call(kernel, message, [SMEM] + [VMEM] * 4, work)(blk, weight, slot, child_field, send_list)
        return lax.ppermute(msg, "blk", pairs)

    last = size - 1
    down = [(i, i - 1) for i in range(1, last)]
    across = [(i, i + 1) for i in range(1, last - 1)] + [(last, 0), (0, last)]
    rest = [(0, 1), (last - 1, last), (last, last - 1)]
    m1 = trade(lambda i: 1 + 0 * i, down)
    p2 = trade(lambda i: 4 + 0 * i, [(i, (i + 2) % size) for i in range(size)])
    f1 = trade(lambda i: jnp.where(i == 0, 1, 3), across)
    m2 = trade(lambda i: 0 * i, [(i, (i - 2) % size) for i in range(size)])
    g1 = trade(lambda i: jnp.where(i == last, 1, 3), rest)
    own, wide = call(
        own_kernel, [struct((CELLS, channels)), struct((CELLS, LANES))], [VMEM] * 5, 2 * work
    )(weight, slot, child_field, send_list, theta)
    row, narrow = struct((PCOL, channels)), struct((PR, channels))
    restricted, chip, side, tail, head = call(
        gather_kernel, [struct((CELLS, channels)), row, row, narrow, narrow], [SMEM] + [VMEM] * 6, work
    )(grp, own, m1, p2, f1, m2, g1)
    side = swap_open(side, "grp", 1)
    left = lax.ppermute(tail, "blk", [(i, i + 1) for i in range(last)])
    right = lax.ppermute(head, "blk", [(i + 1, i) for i in range(last)])
    chip = swap_open(chip, "grp", 0)
    out = call(final_kernel, struct((CELLS, channels)), [SMEM] + [VMEM] * 6, work)(
        grp, restricted, wide, chip, side, left, right
    )
    return out.reshape(PR, PCOL, channels)


def solution(mesh):
    return jax.shard_map(
        body,
        mesh=mesh,
        in_specs=(
            P(("grp", "blk"), None),
            P(("grp", "blk")),
            P(("grp", "blk")),
            P(("grp", "blk"), None),
            P("grp", "blk"),
        ),
        out_specs=P("grp", "blk", None),
        check_vma=False,
    )
```

time: 55.6 us -> 53.5 us (0.962)
  the two profiles are of different devices: /device:TPU:49 before, /device:TPU:16 now
where the time goes in v2:
time: 53.5 us; the launch traced here: 53.1 us
  starting transfers between devices  37.6 us (70%)
  waiting for transfers between devices  9.79 us (18%)
  Pallas kernels  3.66 us (7%)
  local copies, waits for them, and re-layouts  1.85 us (3%)
    ppermute x5, starting transfers between devices, trade(): return lax.ppermute(msg, 'blk', pairs)  28.5 us
    ppermute x5, waiting for transfers between devices, trade(): return lax.ppermute(msg, 'blk', pairs)  5.5 us
    ppermute x2, starting transfers between devices, swap_open(): return lax.ppermute(x, axis, pairs)  5.25 us
    ppermute x1, waiting for transfers between devices, body(): right = lax.ppermute(head, 'blk', [(i + 1, i) for i in range(last)])  4.2 us
    ppermute x1, starting transfers between devices, body(): left = lax.ppermute(tail, 'blk', [(i, i + 1) for i in range(last)])  2.61 us
    unnamed x12, local copies, waits for them, and re-layouts  1.85 us
    pallas_call x5, Pallas kernels, trade(): call(kernel, message, [SMEM] + [VMEM] * 4, work)  1.49 us
    ppermute x1, starting transfers between devices, body(): right = lax.ppermute(head, 'blk', [(i + 1, i) for i in range(last)])  1.29 us
  transfers between devices with their start and end apart: 9, of which 5 were waited for; matrix products, arithmetic and copies ran while one was open for 0% of the time, Pallas kernels for 3%

profile of v2, /device:TPU:16, one launch (start us, length us, event | category | flops | bytes accessed | tf_op | source)
XLA Modules:
  0.0 53.1 jit_solution(1087153748172620101)
XLA Ops:
  0.0 0.7 %copy-done.4 = bf16[1024]{0:T(1024)(128)(2,1)S(1)} copy-done((bf16[1024]{0:T(1024)(128)(2,1)S(1)}, bf16[1024]{0:T(1024)(128)(2,1)}, u32[]{:S(2)}) %copy-start.4) | copy-done | bytes 2072
  0.7 1.1 %copy-done = bf16[1024,384]{1,0:T(8,128)(2,1)S(1)} copy-done((bf16[1024,384]{1,0:T(8,128)(2,1)S(1)}, bf16[1024,384]{1,0:T(8,128)(2,1)}, u32[]{:S(2)}) %copy-start) | copy-done | bytes 786456
  1.8 0.3 shard_map.56
  2.1 1.3 %collective-permute-start = (f32[392,128]{1,0:T(8,128)S(1)}, f32[392,128]{1,0:T(8,128)S(1)}, u32[]{:S(2)}, u32[]{:S(2)}) collective-permute-start(f32[392,128]{1,0:T(8,128)S(1)} %shard_map.56), channel_id=1, source_target_pairs={{1,0},{2,1},{3,2},{4,3},{5,4},{6,5},{7,6},{8,7},{9,8},{10,9},{11,1... | collective-permute-start | bytes 602120 | tf_op jit(solution)/shard_map/ppermute | solution.py:144
  3.4 0.3 shard_map.57
  3.8 5.5 %collective-permute-start.1 = (f32[392,128]{1,0:T(8,128)S(1)}, f32[392,128]{1,0:T(8,128)S(1)}, u32[]{:S(2)}, u32[]{:S(2)}) collective-permute-start(f32[392,128]{1,0:T(8,128)S(1)} %shard_map.57), channel_id=1, source_target_pairs={{0,2},{1,3},{2,4},{3,5},{4,6},{5,7},{6,8},{7,9},{8,10},{9,11},{10,... | collective-permute-start | bytes 602120 | tf_op jit(solution)/shard_map/ppermute | solution.py:144
  9.2 0.3 shard_map.58
  9.6 15.6 %collective-permute-start.2 = (f32[392,128]{1,0:T(8,128)S(1)}, f32[392,128]{1,0:T(8,128)S(1)}, u32[]{:S(2)}, u32[]{:S(2)}) collective-permute-start(f32[392,128]{1,0:T(8,128)S(1)} %shard_map.58), channel_id=1, source_target_pairs={{1,2},{2,3},{3,4},{4,5},{5,6},{6,7},{7,8},{8,9},{9,10},{10,11},{11... | collective-permute-start | bytes 602120 | tf_op jit(solution)/shard_map/ppermute | solution.py:144
  25.1 0.3 shard_map.59
  25.4 4.8 %collective-permute-start.3 = (f32[392,128]{1,0:T(8,128)S(1)}, f32[392,128]{1,0:T(8,128)S(1)}, u32[]{:S(2)}, u32[]{:S(2)}) collective-permute-start(f32[392,128]{1,0:T(8,128)S(1)} %shard_map.59), channel_id=1, source_target_pairs={{0,62},{1,63},{2,0},{3,1},{4,2},{5,3},{6,4},{7,5},{8,6},{9,7},{10,... | collective-permute-start | bytes 602120 | tf_op jit(solution)/shard_map/ppermute | solution.py:144
  30.3 0.3 shard_map.60
  30.6 1.3 %collective-permute-start.4 = (f32[392,128]{1,0:T(8,128)S(1)}, f32[392,128]{1,0:T(8,128)S(1)}, u32[]{:S(2)}, u32[]{:S(2)}) collective-permute-start(f32[392,128]{1,0:T(8,128)S(1)} %shard_map.60), channel_id=1, source_target_pairs={{0,1},{62,63},{63,62},{64,65},{126,127},{127,126},{128,129},{190,1... | collective-permute-start | bytes 602120 | tf_op jit(solution)/shard_map/ppermute | solution.py:144
  31.9 0.6 %shard_map.55 = (f32[256,384]{1,0:T(8,128)S(1)}, f32[256,128]{1,0:T(8,128)S(1)}) custom-call(bf16[8,128]{1,0:T(8,128)(2,1)S(1)} %bitcast.16, s32[8,128]{1,0:T(8,128)S(1)} %bitcast.10, bf16[1024,384]{1,0:T(8,128)(2,1)S(1)} %copy-done.1, s32[1,640]{1,0:T(1,128)S(1)} %copy-done.3, f32[8,32]{1,0:T(8,128)S(1)} %copy-done.5), custom_call_target="tpu_custom_call" | custom-call | flops 201326592 | bytes 1000000 | tf_op jit(solution)/shard_map/pallas_call | solution.py:155
  32.5 1.6 %collective-permute-done.1.refs_1_ = f32[392,128]{1,0:T(8,128)S(1)} collective-permute-done((f32[392,128]{1,0:T(8,128)S(1)}, f32[392,128]{1,0:T(8,128)S(1)}, u32[]{:S(2)}, u32[]{:S(2)}) %collective-permute-start.1) | collective-permute-done | bytes 200736 | tf_op jit(solution)/shard_map/ppermute | solution.py:144
  34.1 2.2 %collective-permute-done.2.refs_2_ = f32[392,128]{1,0:T(8,128)S(1)} collective-permute-done((f32[392,128]{1,0:T(8,128)S(1)}, f32[392,128]{1,0:T(8,128)S(1)}, u32[]{:S(2)}, u32[]{:S(2)}) %collective-permute-start.2) | collective-permute-done | bytes 200736 | tf_op jit(solution)/shard_map/ppermute | solution.py:144
  36.3 1.7 %collective-permute-done.3.refs_3_ = f32[392,128]{1,0:T(8,128)S(1)} collective-permute-done((f32[392,128]{1,0:T(8,128)S(1)}, f32[392,128]{1,0:T(8,128)S(1)}, u32[]{:S(2)}, u32[]{:S(2)}) %collective-permute-start.3) | collective-permute-done | bytes 200736 | tf_op jit(solution)/shard_map/ppermute | solution.py:144
  38.0 0.7 %shard_map.61 = (f32[256,384]{1,0:T(8,128)S(1)}, f32[32,384]{1,0:T(8,128)S(1)}, f32[32,384]{1,0:T(8,128)S(1)}, f32[8,384]{1,0:T(8,128)S(1)}, f32[8,384]{1,0:T(8,128)S(1)}) custom-call(s32[1]{0:T(128)} %bitcast.grp_ref, f32[256,384]{1,0:T(8,128)S(1)} %get-tuple-element.12.own_ref, f32[392,128]{1,0:T(8,128)S(1)} %collective-permute-done.refs_0_, ...), custom_call_target="tpu_custom_call" | custom-call | flops 100663296 | bytes 1000000 | tf_op jit(solution)/shard_map/pallas_call | solution.py:159
  38.7 1.9 %collective-permute-start.5 = (f32[32,384]{1,0:T(8,128)S(1)}, f32[32,384]{1,0:T(8,128)S(1)}, u32[]{:S(2)}, u32[]{:S(2)}) collective-permute-start(f32[32,384]{1,0:T(8,128)S(1)} %get-tuple-element.15), channel_id=1, source_target_pairs={{0,64},{64,0},{128,192},{192,128},{256,320},{320,256},{384,448},{4... | collective-permute-start | bytes 147464 | tf_op jit(solution)/shard_map/ppermute | solution.py:29
  40.6 3.3 %collective-permute-start.6 = (f32[32,384]{1,0:T(8,128)S(1)}, f32[32,384]{1,0:T(8,128)S(1)}, u32[]{:S(2)}, u32[]{:S(2)}) collective-permute-start(f32[32,384]{1,0:T(8,128)S(1)} %get-tuple-element.16), channel_id=1, source_target_pairs={{64,128},{128,64},{192,256},{256,192},{320,384},{384,320},{448,512... | collective-permute-start | bytes 147464 | tf_op jit(solution)/shard_map/ppermute | solution.py:29
  44.0 2.6 %collective-permute-start.7 = (f32[8,384]{1,0:T(8,128)S(1)}, f32[8,384]{1,0:T(8,128)S(1)}, u32[]{:S(2)}, u32[]{:S(2)}) collective-permute-start(f32[8,384]{1,0:T(8,128)S(1)} %get-tuple-element.17), channel_id=1, source_target_pairs={{0,1},{1,2},{2,3},{3,4},{4,5},{5,6},{6,7},{7,8},{8,9},{9,10},{10,1... | collective-permute-start | bytes 36872 | tf_op jit(solution)/shard_map/ppermute | solution.py:163
  46.6 1.3 %collective-permute-start.8 = (f32[8,384]{1,0:T(8,128)S(1)}, f32[8,384]{1,0:T(8,128)S(1)}, u32[]{:S(2)}, u32[]{:S(2)}) collective-permute-start(f32[8,384]{1,0:T(8,128)S(1)} %get-tuple-element.18), channel_id=1, source_target_pairs={{1,0},{2,1},{3,2},{4,3},{5,4},{6,5},{7,6},{8,7},{9,8},{10,9},{11,1... | collective-permute-start | bytes 36872 | tf_op jit(solution)/shard_map/ppermute | solution.py:164
  47.9 0.1 collective-permute-done.7.left_ref
  48.0 4.2 %collective-permute-done.8.right_ref = f32[8,384]{1,0:T(8,128)S(1)} collective-permute-done((f32[8,384]{1,0:T(8,128)S(1)}, f32[8,384]{1,0:T(8,128)S(1)}, u32[]{:S(2)}, u32[]{:S(2)}) %collective-permute-start.8) | collective-permute-done | bytes 12320 | tf_op jit(solution)/shard_map/ppermute | solution.py:164
  52.2 0.9 %shard_map.62 = f32[256,384]{1,0:T(8,128)} custom-call(s32[1]{0:T(128)} %bitcast.grp_ref, f32[256,384]{1,0:T(8,128)S(1)} %get-tuple-element.13.own_ref, f32[256,128]{1,0:T(8,128)S(1)} %get-tuple-element.14.wide_ref, f32[32,384]{1,0:T(8,128)S(1)} %collective-permute-done.5.chip_ref, f32[32,384]{1,0:T(8,128)S(1)} %collective-permute-done.6.side_ref, ...), custom_call_target="tpu_custom_call" | custom-call | flops 100663296 | bytes 1000000 | tf_op jit(solution)/shard_map/pallas_call | solution.py:166
  (14 shorter events, 0.1 us)
Async XLA Ops:
  0.0 0.7 %copy-start.4 = (bf16[1024]{0:T(1024)(128)(2,1)S(1)}, bf16[1024]{0:T(1024)(128)(2,1)}, u32[]{:S(2)}) copy-start(bf16[1024]{0:T(1024)(128)(2,1)} %param.6) | copy-start | bytes 6148
  0.0 0.7 %copy-start.2 = (s32[1024]{0:T(1024)S(1)}, s32[1024]{0:T(1024)}, u32[]{:S(2)}) copy-start(s32[1024]{0:T(1024)} %param.7) | copy-start | bytes 12292
  0.0 0.7 %copy-start.3 = (s32[1,640]{1,0:T(1,128)S(1)}, s32[1,640]{1,0:T(1,128)}, u32[]{:S(2)}) copy-start(s32[1,640]{1,0:T(1,128)} %list_ref.11) | copy-start | bytes 7684
  0.7 1.1 %copy-start = (bf16[1024,384]{1,0:T(8,128)(2,1)S(1)}, bf16[1024,384]{1,0:T(8,128)(2,1)}, u32[]{:S(2)}) copy-start(bf16[1024,384]{1,0:T(8,128)(2,1)} %field_ref.11) | copy-start | bytes 2359300
  2.1 30.4 %collective-permute-start = (f32[392,128]{1,0:T(8,128)S(1)}, f32[392,128]{1,0:T(8,128)S(1)}, u32[]{:S(2)}, u32[]{:S(2)}) collective-permute-start(f32[392,128]{1,0:T(8,128)S(1)} %shard_map.56), channel_id=1, source_target_pairs={{1,0},{2,1},{3,2},{4,3},{5,4},{6,5},{7,6},{8,7},{9,8},{10,9},{11,1... | collective-permute-start | bytes 602120 | tf_op jit(solution)/shard_map/ppermute | solution.py:144
  3.8 30.4 %collective-permute-start.1 = (f32[392,128]{1,0:T(8,128)S(1)}, f32[392,128]{1,0:T(8,128)S(1)}, u32[]{:S(2)}, u32[]{:S(2)}) collective-permute-start(f32[392,128]{1,0:T(8,128)S(1)} %shard_map.57), channel_id=1, source_target_pairs={{0,2},{1,3},{2,4},{3,5},{4,6},{5,7},{6,8},{7,9},{8,10},{9,11},{10,... | collective-permute-start | bytes 602120 | tf_op jit(solution)/shard_map/ppermute | solution.py:144
  9.5 22.4 %copy-start.1 = (bf16[1024,384]{1,0:T(8,128)(2,1)S(1)}, bf16[1024,384]{1,0:T(8,128)(2,1)}, u32[]{:S(2)}) copy-start(bf16[1024,384]{1,0:T(8,128)(2,1)} %field_ref.11) | copy-start | bytes 2359300
  9.6 26.8 %collective-permute-start.2 = (f32[392,128]{1,0:T(8,128)S(1)}, f32[392,128]{1,0:T(8,128)S(1)}, u32[]{:S(2)}, u32[]{:S(2)}) collective-permute-start(f32[392,128]{1,0:T(8,128)S(1)} %shard_map.58), channel_id=1, source_target_pairs={{1,2},{2,3},{3,4},{4,5},{5,6},{6,7},{7,8},{8,9},{9,10},{10,11},{11... | collective-permute-start | bytes 602120 | tf_op jit(solution)/shard_map/ppermute | solution.py:144
  25.4 12.6 %collective-permute-start.3 = (f32[392,128]{1,0:T(8,128)S(1)}, f32[392,128]{1,0:T(8,128)S(1)}, u32[]{:S(2)}, u32[]{:S(2)}) collective-permute-start(f32[392,128]{1,0:T(8,128)S(1)} %shard_map.59), channel_id=1, source_target_pairs={{0,62},{1,63},{2,0},{3,1},{4,2},{5,3},{6,4},{7,5},{8,6},{9,7},{10,... | collective-permute-start | bytes 602120 | tf_op jit(solution)/shard_map/ppermute | solution.py:144
  30.6 1.3 %copy-start.5 = (f32[8,32]{1,0:T(8,128)S(1)}, f32[8,32]{1,0:T(8,128)}, u32[]{:S(2)}) copy-start(f32[8,32]{1,0:T(8,128)} %theta_ref.1) | copy-start | bytes 3076
  30.6 7.4 %collective-permute-start.4 = (f32[392,128]{1,0:T(8,128)S(1)}, f32[392,128]{1,0:T(8,128)S(1)}, u32[]{:S(2)}, u32[]{:S(2)}) collective-permute-start(f32[392,128]{1,0:T(8,128)S(1)} %shard_map.60), channel_id=1, source_target_pairs={{0,1},{62,63},{63,62},{64,65},{126,127},{127,126},{128,129},{190,1... | collective-permute-start | bytes 602120 | tf_op jit(solution)/shard_map/ppermute | solution.py:144
  38.7 13.5 %collective-permute-start.5 = (f32[32,384]{1,0:T(8,128)S(1)}, f32[32,384]{1,0:T(8,128)S(1)}, u32[]{:S(2)}, u32[]{:S(2)}) collective-permute-start(f32[32,384]{1,0:T(8,128)S(1)} %get-tuple-element.15), channel_id=1, source_target_pairs={{0,64},{64,0},{128,192},{192,128},{256,320},{320,256},{384,448},{4... | collective-permute-start | bytes 147464 | tf_op jit(solution)/shard_map/ppermute | solution.py:29
  40.6 11.6 %collective-permute-start.6 = (f32[32,384]{1,0:T(8,128)S(1)}, f32[32,384]{1,0:T(8,128)S(1)}, u32[]{:S(2)}, u32[]{:S(2)}) collective-permute-start(f32[32,384]{1,0:T(8,128)S(1)} %get-tuple-element.16), channel_id=1, source_target_pairs={{64,128},{128,64},{192,256},{256,192},{320,384},{384,320},{448,512... | collective-permute-start | bytes 147464 | tf_op jit(solution)/shard_map/ppermute | solution.py:29
  44.0 4.0 %collective-permute-start.7 = (f32[8,384]{1,0:T(8,128)S(1)}, f32[8,384]{1,0:T(8,128)S(1)}, u32[]{:S(2)}, u32[]{:S(2)}) collective-permute-start(f32[8,384]{1,0:T(8,128)S(1)} %get-tuple-element.17), channel_id=1, source_target_pairs={{0,1},{1,2},{2,3},{3,4},{4,5},{5,6},{6,7},{7,8},{8,9},{9,10},{10,1... | collective-permute-start | bytes 36872 | tf_op jit(solution)/shard_map/ppermute | solution.py:163
  46.6 5.6 %collective-permute-start.8 = (f32[8,384]{1,0:T(8,128)S(1)}, f32[8,384]{1,0:T(8,128)S(1)}, u32[]{:S(2)}, u32[]{:S(2)}) collective-permute-start(f32[8,384]{1,0:T(8,128)S(1)} %get-tuple-element.18), channel_id=1, source_target_pairs={{1,0},{2,1},{3,2},{4,3},{5,4},{6,5},{7,6},{8,7},{9,8},{10,9},{11,1... | collective-permute-start | bytes 36872 | tf_op jit(solution)/shard_map/ppermute | solution.py:164

commit v3 on v2

--- a/solution.py
+++ b/solution.py
@@ -144,12 +144,12 @@
         return lax.ppermute(msg, "blk", pairs)
 
     last = size - 1
-    down = [(i, i - 1) for i in range(1, last)]
-    across = [(i, i + 1) for i in range(1, last - 1)] + [(last, 0), (0, last)]
-    rest = [(0, 1), (last - 1, last), (last, last - 1)]
+    down = [(i, i - 1) for i in range(1, last - 1)]
+    across = [(i, i + 1) for i in (*range(1, last - 3), last - 2)] + [(last, 0), (0, last), (last - 1, last - 2)]
+    rest = [(0, 1), (last - 3, last - 2), (last - 1, last), (last, last - 1)]
+    p2 = trade(lambda i: 4 + 0 * i, [(i, (i + 2) % size) for i in range(size)])
     m1 = trade(lambda i: 1 + 0 * i, down)
-    p2 = trade(lambda i: 4 + 0 * i, [(i, (i + 2) % size) for i in range(size)])
-    f1 = trade(lambda i: jnp.where(i == 0, 1, 3), across)
+    f1 = trade(lambda i: jnp.where((i == 0) | (i == last - 1), 1, 3), across)
     m2 = trade(lambda i: 0 * i, [(i, (i - 2) % size) for i in range(size)])
     g1 = trade(lambda i: jnp.where(i == last, 1, 3), rest)
     own, wide = call(

time: 53.5 us -> 55.3 us (1.034)
  the two profiles are of different devices: /device:TPU:16 before, /device:TPU:49 now
where the time goes in v3:
time: 55.3 us; the launch traced here: 54.9 us
  starting transfers between devices  42.3 us (76%)
  waiting for transfers between devices  6.93 us (13%)
  Pallas kernels  3.66 us (7%)
  local copies, waits for them, and re-layouts  1.85 us (3%)
    ppermute x5, starting transfers between devices, trade(): return lax.ppermute(msg, 'blk', pairs)  29.7 us
    ppermute x2, starting transfers between devices, swap_open(): return lax.ppermute(x, axis, pairs)  8.65 us
    ppermute x5, waiting for transfers between devices, trade(): return lax.ppermute(msg, 'blk', pairs)  3.79 us
    ppermute x1, waiting for transfers between devices, body(): right = lax.ppermute(head, 'blk', [(i + 1, i) for i in range(last)])  3.13 us
    ppermute x1, starting transfers between devices, body(): left = lax.ppermute(tail, 'blk', [(i, i + 1) for i in range(last)])  2.65 us
    unnamed x12, local copies, waits for them, and re-layouts  1.85 us
    pallas_call x5, Pallas kernels, trade(): call(kernel, message, [SMEM] + [VMEM] * 4, work)  1.49 us
    ppermute x1, starting transfers between devices, body(): right = lax.ppermute(head, 'blk', [(i + 1, i) for i in range(last)])  1.29 us
  transfers between devices with their start and end apart: 9, of which 3 were waited for; matrix products, arithmetic and copies ran while one was open for 0% of the time, Pallas kernels for 3%

profile of v3, /device:TPU:49, one launch (start us, length us, event | category | flops | bytes accessed | tf_op | source)
XLA Modules:
  0.0 54.9 jit_solution(16936871620014558628)
XLA Ops:
  0.0 0.7 %copy-done.4 = bf16[1024]{0:T(1024)(128)(2,1)S(1)} copy-done((bf16[1024]{0:T(1024)(128)(2,1)S(1)}, bf16[1024]{0:T(1024)(128)(2,1)}, u32[]{:S(2)}) %copy-start.4) | copy-done | bytes 2072
  0.7 0.0 copy-done.2
  0.7 0.0 copy-done.3
  0.7 1.1 %copy-done = bf16[1024,384]{1,0:T(8,128)(2,1)S(1)} copy-done((bf16[1024,384]{1,0:T(8,128)(2,1)S(1)}, bf16[1024,384]{1,0:T(8,128)(2,1)}, u32[]{:S(2)}) %copy-start) | copy-done | bytes 786456
  1.8 0.3 shard_map.56
  2.1 1.3 %collective-permute-start = (f32[392,128]{1,0:T(8,128)S(1)}, f32[392,128]{1,0:T(8,128)S(1)}, u32[]{:S(2)}, u32[]{:S(2)}) collective-permute-start(f32[392,128]{1,0:T(8,128)S(1)} %shard_map.56), channel_id=1, source_target_pairs={{1,0},{2,1},{3,2},{4,3},{5,4},{6,5},{7,6},{8,7},{9,8},{10,9},{11,1... | collective-permute-start | bytes 602120 | tf_op jit(solution)/shard_map/ppermute | solution.py:144
  3.4 0.3 shard_map.57
  3.8 4.9 %collective-permute-start.1 = (f32[392,128]{1,0:T(8,128)S(1)}, f32[392,128]{1,0:T(8,128)S(1)}, u32[]{:S(2)}, u32[]{:S(2)}) collective-permute-start(f32[392,128]{1,0:T(8,128)S(1)} %shard_map.57), channel_id=1, source_target_pairs={{0,2},{1,3},{2,4},{3,5},{4,6},{5,7},{6,8},{7,9},{8,10},{9,11},{10,... | collective-permute-start | bytes 602120 | tf_op jit(solution)/shard_map/ppermute | solution.py:144
  8.7 0.3 shard_map.58
  9.0 15.9 %collective-permute-start.2 = (f32[392,128]{1,0:T(8,128)S(1)}, f32[392,128]{1,0:T(8,128)S(1)}, u32[]{:S(2)}, u32[]{:S(2)}) collective-permute-start(f32[392,128]{1,0:T(8,128)S(1)} %shard_map.58), channel_id=1, source_target_pairs={{1,2},{2,3},{3,4},{4,5},{5,6},{6,7},{7,8},{8,9},{9,10},{10,11},{11... | collective-permute-start | bytes 602120 | tf_op jit(solution)/shard_map/ppermute | solution.py:144
  24.9 0.3 shard_map.59
  25.2 6.3 %collective-permute-start.3 = (f32[392,128]{1,0:T(8,128)S(1)}, f32[392,128]{1,0:T(8,128)S(1)}, u32[]{:S(2)}, u32[]{:S(2)}) collective-permute-start(f32[392,128]{1,0:T(8,128)S(1)} %shard_map.59), channel_id=1, source_target_pairs={{0,62},{1,63},{2,0},{3,1},{4,2},{5,3},{6,4},{7,5},{8,6},{9,7},{10,... | collective-permute-start | bytes 602120 | tf_op jit(solution)/shard_map/ppermute | solution.py:144
  31.5 0.3 shard_map.60
  31.8 1.3 %collective-permute-start.4 = (f32[392,128]{1,0:T(8,128)S(1)}, f32[392,128]{1,0:T(8,128)S(1)}, u32[]{:S(2)}, u32[]{:S(2)}) collective-permute-start(f32[392,128]{1,0:T(8,128)S(1)} %shard_map.60), channel_id=1, source_target_pairs={{0,1},{60,61},{62,63},{63,62},{64,65},{124,125},{126,127},{127,126... | collective-permute-start | bytes 602120 | tf_op jit(solution)/shard_map/ppermute | solution.py:144
  33.2 0.6 %shard_map.55 = (f32[256,384]{1,0:T(8,128)S(1)}, f32[256,128]{1,0:T(8,128)S(1)}) custom-call(bf16[8,128]{1,0:T(8,128)(2,1)S(1)} %bitcast.16, s32[8,128]{1,0:T(8,128)S(1)} %bitcast.10, bf16[1024,384]{1,0:T(8,128)(2,1)S(1)} %copy-done.1, s32[1,640]{1,0:T(1,128)S(1)} %copy-done.3, f32[8,32]{1,0:T(8,128)S(1)} %copy-done.5), custom_call_target="tpu_custom_call" | custom-call | flops 201326592 | bytes 1000000 | tf_op jit(solution)/shard_map/pallas_call | solution.py:155
  33.7 2.1 %collective-permute-done.2.refs_2_ = f32[392,128]{1,0:T(8,128)S(1)} collective-permute-done((f32[392,128]{1,0:T(8,128)S(1)}, f32[392,128]{1,0:T(8,128)S(1)}, u32[]{:S(2)}, u32[]{:S(2)}) %collective-permute-start.2) | collective-permute-done | bytes 200736 | tf_op jit(solution)/shard_map/ppermute | solution.py:144
  35.8 1.7 %collective-permute-done.3.refs_3_ = f32[392,128]{1,0:T(8,128)S(1)} collective-permute-done((f32[392,128]{1,0:T(8,128)S(1)}, f32[392,128]{1,0:T(8,128)S(1)}, u32[]{:S(2)}, u32[]{:S(2)}) %collective-permute-start.3) | collective-permute-done | bytes 200736 | tf_op jit(solution)/shard_map/ppermute | solution.py:144
  37.5 0.7 %shard_map.61 = (f32[256,384]{1,0:T(8,128)S(1)}, f32[32,384]{1,0:T(8,128)S(1)}, f32[32,384]{1,0:T(8,128)S(1)}, f32[8,384]{1,0:T(8,128)S(1)}, f32[8,384]{1,0:T(8,128)S(1)}) custom-call(s32[1]{0:T(128)} %bitcast.grp_ref, f32[256,384]{1,0:T(8,128)S(1)} %get-tuple-element.12.own_ref, f32[392,128]{1,0:T(8,128)S(1)} %collective-permute-done.refs_0_, ...), custom_call_target="tpu_custom_call" | custom-call | flops 100663296 | bytes 1000000 | tf_op jit(solution)/shard_map/pallas_call | solution.py:159
  38.2 4.1 %collective-permute-start.5 = (f32[32,384]{1,0:T(8,128)S(1)}, f32[32,384]{1,0:T(8,128)S(1)}, u32[]{:S(2)}, u32[]{:S(2)}) collective-permute-start(f32[32,384]{1,0:T(8,128)S(1)} %get-tuple-element.15), channel_id=1, source_target_pairs={{0,64},{64,0},{128,192},{192,128},{256,320},{320,256},{384,448},{4... | collective-permute-start | bytes 147464 | tf_op jit(solution)/shard_map/ppermute | solution.py:29
  42.4 4.5 %collective-permute-start.6 = (f32[32,384]{1,0:T(8,128)S(1)}, f32[32,384]{1,0:T(8,128)S(1)}, u32[]{:S(2)}, u32[]{:S(2)}) collective-permute-start(f32[32,384]{1,0:T(8,128)S(1)} %get-tuple-element.16), channel_id=1, source_target_pairs={{64,128},{128,64},{192,256},{256,192},{320,384},{384,320},{448,512... | collective-permute-start | bytes 147464 | tf_op jit(solution)/shard_map/ppermute | solution.py:29
  46.9 2.7 %collective-permute-start.7 = (f32[8,384]{1,0:T(8,128)S(1)}, f32[8,384]{1,0:T(8,128)S(1)}, u32[]{:S(2)}, u32[]{:S(2)}) collective-permute-start(f32[8,384]{1,0:T(8,128)S(1)} %get-tuple-element.17), channel_id=1, source_target_pairs={{0,1},{1,2},{2,3},{3,4},{4,5},{5,6},{6,7},{7,8},{8,9},{9,10},{10,1... | collective-permute-start | bytes 36872 | tf_op jit(solution)/shard_map/ppermute | solution.py:163
  49.6 1.3 %collective-permute-start.8 = (f32[8,384]{1,0:T(8,128)S(1)}, f32[8,384]{1,0:T(8,128)S(1)}, u32[]{:S(2)}, u32[]{:S(2)}) collective-permute-start(f32[8,384]{1,0:T(8,128)S(1)} %get-tuple-element.18), channel_id=1, source_target_pairs={{1,0},{2,1},{3,2},{4,3},{5,4},{6,5},{7,6},{8,7},{9,8},{10,9},{11,1... | collective-permute-start | bytes 36872 | tf_op jit(solution)/shard_map/ppermute | solution.py:164
  50.9 3.1 %collective-permute-done.8.right_ref = f32[8,384]{1,0:T(8,128)S(1)} collective-permute-done((f32[8,384]{1,0:T(8,128)S(1)}, f32[8,384]{1,0:T(8,128)S(1)}, u32[]{:S(2)}, u32[]{:S(2)}) %collective-permute-start.8) | collective-permute-done | bytes 12320 | tf_op jit(solution)/shard_map/ppermute | solution.py:164
  54.0 0.9 %shard_map.62 = f32[256,384]{1,0:T(8,128)} custom-call(s32[1]{0:T(128)} %bitcast.grp_ref, f32[256,384]{1,0:T(8,128)S(1)} %get-tuple-element.13.own_ref, f32[256,128]{1,0:T(8,128)S(1)} %get-tuple-element.14.wide_ref, f32[32,384]{1,0:T(8,128)S(1)} %collective-permute-done.5.chip_ref, f32[32,384]{1,0:T(8,128)S(1)} %collective-permute-done.6.side_ref, ...), custom_call_target="tpu_custom_call" | custom-call | flops 100663296 | bytes 1000000 | tf_op jit(solution)/shard_map/pallas_call | solution.py:166
  (14 shorter events, 0.0 us)
Async XLA Ops:
  0.0 0.7 %copy-start.4 = (bf16[1024]{0:T(1024)(128)(2,1)S(1)}, bf16[1024]{0:T(1024)(128)(2,1)}, u32[]{:S(2)}) copy-start(bf16[1024]{0:T(1024)(128)(2,1)} %param.6) | copy-start | bytes 6148
  0.0 0.7 %copy-start.2 = (s32[1024]{0:T(1024)S(1)}, s32[1024]{0:T(1024)}, u32[]{:S(2)}) copy-start(s32[1024]{0:T(1024)} %param.7) | copy-start | bytes 12292
  0.0 0.7 %copy-start.3 = (s32[1,640]{1,0:T(1,128)S(1)}, s32[1,640]{1,0:T(1,128)}, u32[]{:S(2)}) copy-start(s32[1,640]{1,0:T(1,128)} %list_ref.11) | copy-start | bytes 7684
  0.7 1.1 %copy-start = (bf16[1024,384]{1,0:T(8,128)(2,1)S(1)}, bf16[1024,384]{1,0:T(8,128)(2,1)}, u32[]{:S(2)}) copy-start(bf16[1024,384]{1,0:T(8,128)(2,1)} %field_ref.11) | copy-start | bytes 2359300
  2.1 31.6 %collective-permute-start = (f32[392,128]{1,0:T(8,128)S(1)}, f32[392,128]{1,0:T(8,128)S(1)}, u32[]{:S(2)}, u32[]{:S(2)}) collective-permute-start(f32[392,128]{1,0:T(8,128)S(1)} %shard_map.56), channel_id=1, source_target_pairs={{1,0},{2,1},{3,2},{4,3},{5,4},{6,5},{7,6},{8,7},{9,8},{10,9},{11,1... | collective-permute-start | bytes 602120 | tf_op jit(solution)/shard_map/ppermute | solution.py:144
  3.8 30.0 %collective-permute-start.1 = (f32[392,128]{1,0:T(8,128)S(1)}, f32[392,128]{1,0:T(8,128)S(1)}, u32[]{:S(2)}, u32[]{:S(2)}) collective-permute-start(f32[392,128]{1,0:T(8,128)S(1)} %shard_map.57), channel_id=1, source_target_pairs={{0,2},{1,3},{2,4},{3,5},{4,6},{5,7},{6,8},{7,9},{8,10},{9,11},{10,... | collective-permute-start | bytes 602120 | tf_op jit(solution)/shard_map/ppermute | solution.py:144
  9.0 24.2 %copy-start.1 = (bf16[1024,384]{1,0:T(8,128)(2,1)S(1)}, bf16[1024,384]{1,0:T(8,128)(2,1)}, u32[]{:S(2)}) copy-start(bf16[1024,384]{1,0:T(8,128)(2,1)} %field_ref.11) | copy-start | bytes 2359300
  9.0 26.8 %collective-permute-start.2 = (f32[392,128]{1,0:T(8,128)S(1)}, f32[392,128]{1,0:T(8,128)S(1)}, u32[]{:S(2)}, u32[]{:S(2)}) collective-permute-start(f32[392,128]{1,0:T(8,128)S(1)} %shard_map.58), channel_id=1, source_target_pairs={{1,2},{2,3},{3,4},{4,5},{5,6},{6,7},{7,8},{8,9},{9,10},{10,11},{11... | collective-permute-start | bytes 602120 | tf_op jit(solution)/shard_map/ppermute | solution.py:144
  25.2 12.4 %collective-permute-start.3 = (f32[392,128]{1,0:T(8,128)S(1)}, f32[392,128]{1,0:T(8,128)S(1)}, u32[]{:S(2)}, u32[]{:S(2)}) collective-permute-start(f32[392,128]{1,0:T(8,128)S(1)} %shard_map.59), channel_id=1, source_target_pairs={{0,62},{1,63},{2,0},{3,1},{4,2},{5,3},{6,4},{7,5},{8,6},{9,7},{10,... | collective-permute-start | bytes 602120 | tf_op jit(solution)/shard_map/ppermute | solution.py:144
  31.8 1.3 %copy-start.5 = (f32[8,32]{1,0:T(8,128)S(1)}, f32[8,32]{1,0:T(8,128)}, u32[]{:S(2)}) copy-start(f32[8,32]{1,0:T(8,128)} %theta_ref.1) | copy-start | bytes 3076
  31.8 5.7 %collective-permute-start.4 = (f32[392,128]{1,0:T(8,128)S(1)}, f32[392,128]{1,0:T(8,128)S(1)}, u32[]{:S(2)}, u32[]{:S(2)}) collective-permute-start(f32[392,128]{1,0:T(8,128)S(1)} %shard_map.60), channel_id=1, source_target_pairs={{0,1},{60,61},{62,63},{63,62},{64,65},{124,125},{126,127},{127,126... | collective-permute-start | bytes 602120 | tf_op jit(solution)/shard_map/ppermute | solution.py:144
  38.2 15.8 %collective-permute-start.5 = (f32[32,384]{1,0:T(8,128)S(1)}, f32[32,384]{1,0:T(8,128)S(1)}, u32[]{:S(2)}, u32[]{:S(2)}) collective-permute-start(f32[32,384]{1,0:T(8,128)S(1)} %get-tuple-element.15), channel_id=1, source_target_pairs={{0,64},{64,0},{128,192},{192,128},{256,320},{320,256},{384,448},{4... | collective-permute-start | bytes 147464 | tf_op jit(solution)/shard_map/ppermute | solution.py:29
  42.4 11.6 %collective-permute-start.6 = (f32[32,384]{1,0:T(8,128)S(1)}, f32[32,384]{1,0:T(8,128)S(1)}, u32[]{:S(2)}, u32[]{:S(2)}) collective-permute-start(f32[32,384]{1,0:T(8,128)S(1)} %get-tuple-element.16), channel_id=1, source_target_pairs={{64,128},{128,64},{192,256},{256,192},{320,384},{384,320},{448,512... | collective-permute-start | bytes 147464 | tf_op jit(solution)/shard_map/ppermute | solution.py:29
  46.9 4.0 %collective-permute-start.7 = (f32[8,384]{1,0:T(8,128)S(1)}, f32[8,384]{1,0:T(8,128)S(1)}, u32[]{:S(2)}, u32[]{:S(2)}) collective-permute-start(f32[8,384]{1,0:T(8,128)S(1)} %get-tuple-element.17), channel_id=1, source_target_pairs={{0,1},{1,2},{2,3},{3,4},{4,5},{5,6},{6,7},{7,8},{8,9},{9,10},{10,1... | collective-permute-start | bytes 36872 | tf_op jit(solution)/shard_map/ppermute | solution.py:163
  49.6 4.4 %collective-permute-start.8 = (f32[8,384]{1,0:T(8,128)S(1)}, f32[8,384]{1,0:T(8,128)S(1)}, u32[]{:S(2)}, u32[]{:S(2)}) collective-permute-start(f32[8,384]{1,0:T(8,128)S(1)} %get-tuple-element.18), channel_id=1, source_target_pairs={{1,0},{2,1},{3,2},{4,3},{5,4},{6,5},{7,6},{8,7},{9,8},{10,9},{11,1... | collective-permute-start | bytes 36872 | tf_op jit(solution)/shard_map/ppermute | solution.py:164
